TPU v7x, 32 devices: a whole 2x2x4 slice. The times are simulated.
32 devices in a mesh: row: 8 (over z, y), col: 4 (over x, core).
Axes of the slice: x: 2, y: 2, z: 4, core: 2. Of those that a mesh axis runs over, the one named last changes fastest.
Arguments:
- features: float32 [32, 3072], P(None, ('row', 'col')), may hold values from -6 to 6
- block: float32 [16, 3072], P(None, ('row', 'col')), may hold values from -6 to 6
Outputs:
- applied: float32 [16, 3072], P(None, ('row', 'col'))
All inputs are finite; a program needn't handle non-finite values.
Results may differ from a plain program's by a relative error of at most 0.006.
Values may be sent and summed in bfloat16 or wider, within the bound.
A program may use at most 64 MiB of HBM per device.

v0:
```python
import math
import jax
import jax.numpy as jnp
from jax import lax
from jax.sharding import PartitionSpec as P


def kernel_rows(row_feat, row_sq, col_feat, col_sq, scale, start, count):
    part = lax.dynamic_slice_in_dim(row_feat, start, count, 1)
    sq_part = lax.dynamic_slice_in_dim(row_sq, start, count, 0)
    inner = jnp.einsum("fi,fj->ij", part, col_feat, precision=lax.Precision.HIGHEST)
    dist = sq_part[:, None] + col_sq[None, :] - 2.0 * inner
    return jnp.exp(-dist / scale).astype(jnp.bfloat16)


def combine(partial_value, owned):
    whole = lax.psum(partial_value, "col")
    return lax.dynamic_slice_in_dim(whole, lax.axis_index("col") * owned, owned, 1)


def full_plan(features, block, row_feat, scale):
    owned = features.shape[1]
    col_feat = lax.all_gather(features, "row", axis=1, tiled=True)
    row_sq = jnp.sum(row_feat * row_feat, axis=0)
    col_sq = jnp.sum(col_feat * col_feat, axis=0)
    rows = row_feat.shape[1]
    step = math.gcd(512, rows)
    count_blocks = rows // step
    starts = jnp.arange(count_blocks, dtype=jnp.int32) * step
    indexes = jnp.arange(count_blocks, dtype=jnp.int32)

    def fetch(index):
        return kernel_rows(row_feat, row_sq, col_feat, col_sq, scale, starts[index], step)

    def first_pass(index):
        tile = fetch(index)
        return (jnp.sum(tile, axis=1, dtype=jnp.float32), jnp.sum(tile, axis=0, dtype=jnp.float32))

    row_parts, col_parts = lax.map(first_pass, indexes)
    q_own = combine(row_parts.reshape(1, rows), owned)
    inv_own = 1.0 / q_own
    col_total = lax.psum(jnp.sum(col_parts, axis=0)[None, :], "row")
    inv_col = 1.0 / col_total

    def second_pass(index):
        return jnp.sum(fetch(index).astype(jnp.float32) * inv_col, axis=1)

    second = combine(lax.map(second_pass, indexes).reshape(1, rows), owned)
    dens = second * inv_own
    factor = inv_own * lax.rsqrt(dens)
    weighted = (block * factor).astype(jnp.bfloat16)
    weighted_col = lax.all_gather(weighted, "row", axis=1, tiled=True)

    def third_pass(index):
        return jnp.einsum(
            "kj,ij->ki", weighted_col, fetch(index), preferred_element_type=jnp.float32
        )

    products = lax.map(third_pass, indexes)
    partial_value = jnp.moveaxis(products, 0, 1).reshape(block.shape[0], rows)
    return combine(partial_value, owned) * factor


def per_device(features, block):
    n_row = lax.axis_size("row")
    n_col = lax.axis_size("col")
    width, owned = features.shape
    frames = owned * n_row * n_col
    scale = 4.0 / (float(frames) ** (2.0 / width) - 1.0)
    row_feat = lax.all_gather(features, "col", axis=1, tiled=True)
    return full_plan(features, block, row_feat, scale)


def solution(mesh):
    placed = (P(None, ("row", "col")), P(None, ("row", "col")))
    return jax.shard_map(
        per_device, mesh=mesh, in_specs=placed, out_specs=P(None, ("row", "col")), check_vma=False
    )
```

profile of v0, /device:TPU:0, one launch (start us, length us, event | category | flops | bytes accessed | tf_op | source)
XLA Modules:
  0.0 166.0 jit_solution(17195008290931523014)
XLA Ops:
  0.0 32.5 %all-gather.1 = f32[8,96,32]{1,2,0:T(8,128)S(1)} all-gather(f32[1,96,32]{1,2,0:T(8,128)} %bitcast.84), channel_id=1, replica_groups=mesh['row'=8,'col'=4] {'row'}, dimensions={0}, use_global_device_ids=true | all-gather | bytes 110592 | tf_op jit(solution)/shard_map/all_gather | solution.py:23
  32.5 0.1 copy.13
  32.6 0.1 reshape.21
  32.8 0.7 copy-done
  33.4 5.2 %all-gather = f32[4,96,32]{1,2,0:T(8,128)S(1)} all-gather(f32[1,96,32]{1,2,0:T(8,128)S(1)} %bitcast.85), channel_id=1, replica_groups=mesh['row'=8,'col'=4] {'col'}, dimensions={0}, use_global_device_ids=true | all-gather | bytes 61440 | tf_op jit(solution)/shard_map/all_gather | solution.py:70
  38.7 0.1 reshape.19
  38.9 19.3 %while.32 = (s32[]{:T(128)}, f32[3,128]{1,0:T(4,128)S(1)}, f32[3,768]{1,0:T(4,128)S(1)}, s32[3]{0:T(128)S(1)}, s32[3]{0:T(128)S(1)}, /*index=5*/f32[384]{0:T(512...) while((s32[]{:T(128)}, f32[3,128]{1,0:T(4,128)S(1)}, ...), condition=%wide.region_5.6_spmd, body=%wide.region_2.5_spmd.sunk | while | flops 38632584 | bytes 137449 | solution.py:39
  38.9 0.7 dynamic_slice.87
  41.6 0.7 dynamic_slice.88
  44.4 0.1 dynamic_slice.89
  44.5 0.7 fusion.51
  45.3 0.7 dynamic_slice.87
  48.1 0.7 dynamic_slice.88
  50.9 0.7 fusion.51
  51.8 0.7 dynamic_slice.87
  54.5 0.7 dynamic_slice.88
  57.3 0.7 fusion.51
  58.2 21.4 %psum.29 = f32[1,768]{1,0:T(1,128)S(1)} all-reduce(f32[1,768]{1,0:T(1,128)S(1)} %broadcast_in_dim.32), channel_id=1, replica_groups=mesh['row'=8,'col'=4] {'row'}, use_global_device_ids=true, to_apply=%region_8.9 | all-reduce | flops 768 | bytes 6144 | tf_op jit(solution)/shard_map/psum | solution.py:42
  79.6 19.1 %while.33 = (s32[]{:T(128)}, f32[3,128]{1,0:T(4,128)S(1)}, s32[3]{0:T(128)S(1)}, s32[3]{0:T(128)S(1)}, f32[384]{0:T(512)S(1)}, /*index=5*/f32[768]{0:T(1024)S(1)...) while((s32[]{:T(128)}, f32[3,128]{1,0:T(4,128)S(1)}, ...), condition=%wide.region_11.12_spmd, body=%wide.region_9.11_spmd.sunk | while | flops 38633352 | bytes 132337 | solution.py:48
  79.6 0.7 dynamic_slice.91
  82.4 0.7 dynamic_slice.92
  85.2 0.7 fusion.54
  86.0 0.7 dynamic_slice.91
  88.7 0.7 dynamic_slice.92
  91.6 0.7 fusion.54
  92.3 0.7 dynamic_slice.91
  95.1 0.7 dynamic_slice.92
  97.9 0.7 fusion.54
  98.7 5.7 %all-reduce = (f32[1,384]{1,0:T(1,128)S(1)}, f32[1,384]{1,0:T(1,128)S(1)}) all-reduce(f32[1,384]{1,0:T(1,128)S(1)} %get-tuple-element.209, f32[1,384]{1,0:T(1,128)S(1)} %get-tuple-element.210), channel_id=1, replica_groups=mesh['row'=8,'col'=4] {'col'}, use_global_device_ids=true, to_apply=%region_12.13 | all-reduce | flops 768 | bytes 6144 | tf_op jit(solution)/shard_map/psum | solution.py:17
  104.5 0.6 copy-done.1
  105.1 30.6 %all-gather.2 = bf16[8,96,16]{1,2,0:T(8,128)(2,1)S(1)} all-gather(bf16[1,96,16]{1,2,0:T(8,128)(2,1)S(1)} %fusion.26), channel_id=1, replica_groups=mesh['row'=8,'col'=4] {'row'}, dimensions={0}, use_global_device_ids=true | all-gather | bytes 27648 | tf_op jit(solution)/shard_map/all_gather | solution.py:52
  135.7 0.1 reshape.23
  135.8 19.2 %while.34 = (s32[]{:T(128)}, f32[3,16,128]{2,1,0:T(8,128)S(1)}, s32[3]{0:T(128)S(1)}, s32[3]{0:T(128)S(1)}, f32[384]{0:T(512)S(1)}, /*index=5*/f32[768]{0:T(1024...) while((s32[]{:T(128)}, f32[3,16,128]{2,1,0:T(8,128)S(1)}, ...), condition=%wide.region_14.15_spmd, body=%wide.region_13.14_spmd.sunk | while | flops 41484296 | bytes 546533 | solution.py:59
  135.8 0.7 dynamic_slice.95
  138.6 0.7 dynamic_slice.96
  141.3 0.1 dynamic_slice.97
  141.4 0.6 fusion.59
  142.0 0.1 fusion.60
  142.2 0.7 dynamic_slice.95
  145.0 0.7 dynamic_slice.96
  147.8 0.6 fusion.59
  148.4 0.1 fusion.60
  148.6 0.7 dynamic_slice.95
  151.4 0.7 dynamic_slice.96
  154.2 0.6 fusion.59
  154.8 0.1 fusion.60
  155.0 10.3 %psum.31 = f32[16,384]{1,0:T(8,128)S(1)} all-reduce(f32[16,384]{1,0:T(8,128)S(1)} %copy_bitcast_fusion), channel_id=1, replica_groups=mesh['row'=8,'col'=4] {'col'}, use_global_device_ids=true, to_apply=%region_15.16 | all-reduce | flops 6144 | bytes 49152 | tf_op jit(solution)/shard_map/psum | solution.py:17
  165.3 0.7 dynamic-slice_multiply_fusion
  (43 shorter events, 1.3 us)
Async XLA Ops:
  32.7 0.7 copy-start
  104.4 0.7 copy-start.1
where the time goes:
time: 167 us; the launch traced here: 166 us
  blocking collectives  106 us (63%)
  loops' own time  37.5 us (22%)
  local copies, waits for them, and re-layouts  15 us (9%)
  matrix products  6.79 us (4%)
    all_gather x1, blocking collectives, full_plan(): col_feat = lax.all_gather(features, 'row', axis=1, tiled=True)  32.5 us
    all_gather x1, blocking collectives, full_plan(): weighted_col = lax.all_gather(weighted, 'row', axis=1, tiled=True)  30.6 us
    psum x1, blocking collectives, full_plan(): col_total = lax.psum(jnp.sum(col_parts, axis=0)[None, :], 'row')  21.4 us
    psum x2, blocking collectives, combine(): whole = lax.psum(partial_value, 'col')  16 us
    another operation x1, loops' own time, full_plan(): row_parts, col_parts = lax.map(first_pass, indexes)  12.5 us
    another operation x1, loops' own time, full_plan(): products = lax.map(third_pass, indexes)  12.5 us
    another operation x1, loops' own time, full_plan(): second = combine(lax.map(second_pass, indexes).reshape(1, rows), owned)  12.5 us
    dot_general x9, matrix products, kernel_rows(): jnp.einsum('fi,fj->ij', part, col_feat, precision=lax.Precision.HIGHEST)  6.41 us

commit v1 on v0

--- a/solution.py
+++ b/solution.py
@@ -39,7 +39,9 @@
     row_parts, col_parts = lax.map(first_pass, indexes)
     q_own = combine(row_parts.reshape(1, rows), owned)
     inv_own = 1.0 / q_own
-    col_total = lax.psum(jnp.sum(col_parts, axis=0)[None, :], "row")
+    block_2 = jnp.sum(col_parts, axis=0)[None, :]
+    parts = lax.all_gather(block_2, "row", axis=0, tiled=False)
+    col_total = parts.sum(axis=0)
     inv_col = 1.0 / col_total
 
     def second_pass(index):

time: 167 us -> 176 us (1.054)
  blocking collectives: 106 us -> 115 us
    all_gather x0 -> x1, blocking collectives: none -> 30.5 us  [full_plan(): parts = lax.all_gather(block_2, 'row', axis=0, tiled=False)]
    psum x1 -> x0, blocking collectives: 21.4 us -> none  [full_plan(): col_total = lax.psum(jnp.sum(col_parts, axis=0)[None, :], 'row')]
where the time goes in v1:
time: 176 us; the launch traced here: 175 us
  blocking collectives  115 us (65%)
  loops' own time  37.5 us (21%)
  local copies, waits for them, and re-layouts  15 us (9%)
  matrix products  6.79 us (4%)
    all_gather x1, blocking collectives, full_plan(): col_feat = lax.all_gather(features, 'row', axis=1, tiled=True)  32.5 us
    all_gather x1, blocking collectives, full_plan(): weighted_col = lax.all_gather(weighted, 'row', axis=1, tiled=True)  30.6 us
    all_gather x1, blocking collectives, full_plan(): parts = lax.all_gather(block_2, 'row', axis=0, tiled=False)  30.5 us
    psum x2, blocking collectives, combine(): whole = lax.psum(partial_value, 'col')  16 us
    another operation x1, loops' own time, full_plan(): row_parts, col_parts = lax.map(first_pass, indexes)  12.5 us
    another operation x1, loops' own time, full_plan(): products = lax.map(third_pass, indexes)  12.5 us
    another operation x1, loops' own time, full_plan(): second = combine(lax.map(second_pass, indexes).reshape(1, rows), owned)  12.5 us
    dot_general x9, matrix products, kernel_rows(): jnp.einsum('fi,fj->ij', part, col_feat, precision=lax.Precision.HIGHEST)  6.41 us

profile of v1, /device:TPU:0, one launch (start us, length us, event | category | flops | bytes accessed | tf_op | source)
XLA Modules:
  0.0 175.2 jit_solution(14692213664940323825)
XLA Ops:
  0.0 32.5 %all-gather.2 = f32[8,96,32]{1,2,0:T(8,128)S(1)} all-gather(f32[1,96,32]{1,2,0:T(8,128)} %bitcast.84), channel_id=1, replica_groups=mesh['row'=8,'col'=4] {'row'}, dimensions={0}, use_global_device_ids=true | all-gather | bytes 110592 | tf_op jit(solution)/shard_map/all_gather | solution.py:23
  32.5 0.1 copy.13
  32.6 0.1 reshape.34
  32.8 0.7 copy-done
  33.4 5.2 %all-gather.1 = f32[4,96,32]{1,2,0:T(8,128)S(1)} all-gather(f32[1,96,32]{1,2,0:T(8,128)S(1)} %bitcast.85), channel_id=1, replica_groups=mesh['row'=8,'col'=4] {'col'}, dimensions={0}, use_global_device_ids=true | all-gather | bytes 61440 | tf_op jit(solution)/shard_map/all_gather | solution.py:72
  38.7 0.1 reshape.32
  38.9 19.3 %while.32 = (s32[]{:T(128)}, f32[3,128]{1,0:T(4,128)S(1)}, f32[3,768]{1,0:T(4,128)S(1)}, s32[3]{0:T(128)S(1)}, s32[3]{0:T(128)S(1)}, /*index=5*/f32[384]{0:T(512...) while((s32[]{:T(128)}, f32[3,128]{1,0:T(4,128)S(1)}, ...), condition=%wide.region_5.6_spmd, body=%wide.region_2.5_spmd.sunk | while | flops 38632584 | bytes 137449 | solution.py:39
  38.9 0.7 dynamic_slice.87
  41.6 0.7 dynamic_slice.88
  44.4 0.1 dynamic_slice.89
  44.5 0.7 fusion.51
  45.3 0.7 dynamic_slice.87
  48.1 0.7 dynamic_slice.88
  50.9 0.7 fusion.51
  51.8 0.7 dynamic_slice.87
  54.5 0.7 dynamic_slice.88
  57.3 0.7 fusion.51
  58.2 30.5 %all-gather.3 = f32[8,1,768]{2,1,0:T(1,128)S(1)} all-gather(f32[1,1,768]{2,1,0:T(1,128)S(1)} %reshape.35), channel_id=2, replica_groups=mesh['row'=8,'col'=4] {'row'}, dimensions={0}, use_global_device_ids=true | all-gather | bytes 27648 | tf_op jit(solution)/shard_map/all_gather | solution.py:43
  88.8 19.1 %while.33 = (s32[]{:T(128)}, f32[3,128]{1,0:T(4,128)S(1)}, s32[3]{0:T(128)S(1)}, s32[3]{0:T(128)S(1)}, f32[384]{0:T(512)S(1)}, /*index=5*/f32[768]{0:T(1024)S(1)...) while((s32[]{:T(128)}, f32[3,128]{1,0:T(4,128)S(1)}, ...), condition=%wide.region_11.12_spmd, body=%wide.region_9.11_spmd.sunk | while | flops 38633352 | bytes 132337 | solution.py:50
  88.8 0.7 dynamic_slice.91
  91.6 0.7 dynamic_slice.92
  94.4 0.7 fusion.54
  95.2 0.7 dynamic_slice.91
  97.9 0.7 dynamic_slice.92
  100.8 0.7 fusion.54
  101.5 0.7 dynamic_slice.91
  104.3 0.7 dynamic_slice.92
  107.1 0.7 fusion.54
  107.9 5.7 %all-reduce = (f32[1,384]{1,0:T(1,128)S(1)}, f32[1,384]{1,0:T(1,128)S(1)}) all-reduce(f32[1,384]{1,0:T(1,128)S(1)} %get-tuple-element.209, f32[1,384]{1,0:T(1,128)S(1)} %get-tuple-element.210), channel_id=1, replica_groups=mesh['row'=8,'col'=4] {'col'}, use_global_device_ids=true, to_apply=%region_12.13 | all-reduce | flops 768 | bytes 6144 | tf_op jit(solution)/shard_map/psum | solution.py:17
  113.7 0.6 copy-done.1
  114.3 30.6 %all-gather.4 = bf16[8,96,16]{1,2,0:T(8,128)(2,1)S(1)} all-gather(bf16[1,96,16]{1,2,0:T(8,128)(2,1)S(1)} %fusion.26), channel_id=1, replica_groups=mesh['row'=8,'col'=4] {'row'}, dimensions={0}, use_global_device_ids=true | all-gather | bytes 27648 | tf_op jit(solution)/shard_map/all_gather | solution.py:54
  144.9 0.1 reshape.38
  145.0 19.2 %while.34 = (s32[]{:T(128)}, f32[3,16,128]{2,1,0:T(8,128)S(1)}, s32[3]{0:T(128)S(1)}, s32[3]{0:T(128)S(1)}, f32[384]{0:T(512)S(1)}, /*index=5*/f32[768]{0:T(1024...) while((s32[]{:T(128)}, f32[3,16,128]{2,1,0:T(8,128)S(1)}, ...), condition=%wide.region_14.15_spmd, body=%wide.region_13.14_spmd.sunk | while | flops 41484296 | bytes 546533 | solution.py:61
  145.0 0.7 dynamic_slice.95
  147.8 0.7 dynamic_slice.96
  150.5 0.1 dynamic_slice.97
  150.6 0.6 fusion.59
  151.2 0.1 fusion.60
  151.4 0.7 dynamic_slice.95
  154.2 0.7 dynamic_slice.96
  157.0 0.6 fusion.59
  157.6 0.1 fusion.60
  157.8 0.7 dynamic_slice.95
  160.6 0.7 dynamic_slice.96
  163.4 0.6 fusion.59
  164.1 0.1 fusion.60
  164.2 10.3 %psum.23 = f32[16,384]{1,0:T(8,128)S(1)} all-reduce(f32[16,384]{1,0:T(8,128)S(1)} %copy_bitcast_fusion), channel_id=1, replica_groups=mesh['row'=8,'col'=4] {'col'}, use_global_device_ids=true, to_apply=%region_15.16 | all-reduce | flops 6144 | bytes 49152 | tf_op jit(solution)/shard_map/psum | solution.py:17
  174.5 0.7 dynamic-slice_multiply_fusion
  (45 shorter events, 1.3 us)
Async XLA Ops:
  32.7 0.7 copy-start
  113.6 0.7 copy-start.1
